TPU v7x, 32 devices: a whole 2x2x4 slice. The times are simulated.
32 devices in a mesh: groups: 1, slab: 8 (over z, y), coil: 2 (over x), row: 2 (over core).
Axes of the slice: x: 2, y: 2, z: 4, core: 2. Of those that a mesh axis runs over, the one named last changes fastest.
Arguments:
- image: float32 [2, 128, 256, 128], P('groups', None, ('slab', 'row')), may hold values from -6 to 6
- sens: bfloat16 [2, 16, 128, 256, 128], P('groups', 'coil', None, ('slab', 'row')), may hold values from -1.5 to 1.5
- measured: bfloat16 [2, 16, 128, 256, 128], P('groups', 'coil', ('slab', 'row')), may hold values from -3 to 3
- mask: int32 [128, 256], P(('slab', 'row')), may hold values from 0 to 1, as said below
- thresholds: float32 [2, 7], replicated, may hold values from 0.1 to 1.5
Outputs:
- image_next: float32 [2, 128, 256, 128], P('groups', None, ('slab', 'row'))
Inputs may be any that keep to these rules, and one draw needn't show every extreme that they name: `mask`: A calibration block of the 8 central phase-encode lines (ky from 60 to 67) is sampled at every kz; outside it each (ky, kz) is sampled independently at random.
All inputs are finite; a program needn't handle non-finite values.
Results may differ from a plain program's by a relative error of at most 0.013.
Values may be sent and summed in bfloat16 or wider, within the bound.
A program may use at most 128 MiB of HBM per device.

v0:
```python
import math
import jax
import jax.numpy as jnp
from jax import lax
from jax.sharding import PartitionSpec as P

half_root = 0.7071067811865476
quarter_root = 0.3535533905932738
step_size = 0.5


def passed_along(block, axis, distance):
    devices = range(lax.axis_size(axis))
    route = [((i - distance) % len(devices), i) for i in devices]
    return lax.ppermute(block, axis, route)


def fourier_table(length, sign):
    index = jnp.arange(length, dtype=jnp.int32)
    phase = index[:, None] * index[None, :] % length
    theta = phase.astype(jnp.float32) * jnp.float32(2.0 * math.pi / length)
    scale = jnp.float32(1.0 / math.sqrt(length))
    real = jnp.cos(theta) * scale
    imaginary = jnp.sin(theta) * (sign * scale)
    upper = jnp.stack([real, -imaginary])
    lower = jnp.stack([imaginary, real])
    return jnp.stack([upper, lower]).astype(jnp.bfloat16)


def contract(form, values, table):
    return jnp.einsum(form, values, table, preferred_element_type=jnp.float32)


def complex_product(left, right):
    return jnp.stack(
        [left[0] * right[0] - left[1] * right[1], left[0] * right[1] + left[1] * right[0]]
    )


def roll_after(values, along, offset):
    return jnp.roll(values, -offset, axis=along)


def roll_before(values, along, offset):
    return jnp.roll(values, offset, axis=along)


def plane_after(values, along, offset):
    border = lax.slice_in_dim(values, 0, offset, axis=along)
    fetched = passed_along(border.astype(jnp.bfloat16), ("slab", "row"), -1).astype(border.dtype)
    remain = lax.slice_in_dim(values, offset, values.shape[along], axis=along)
    return jnp.concatenate([remain, fetched], axis=along)


def plane_before(values, along, offset):
    extent = values.shape[along]
    border = lax.slice_in_dim(values, extent - offset, extent, axis=along)
    fetched = passed_along(border.astype(jnp.bfloat16), ("slab", "row"), 1).astype(border.dtype)
    remain = lax.slice_in_dim(values, 0, extent - offset, axis=along)
    return jnp.concatenate([fetched, remain], axis=along)


def split_bands(bands, along, offset, after):
    moved = after(bands, along, offset)
    return jnp.concatenate([(bands + moved) * half_root, (bands - moved) * half_root], axis=0)


def merge_bands(bands, along, offset, before):
    half = bands.shape[0] // 2
    lower = bands[:half]
    upper = bands[half:]
    return (lower + upper + before(lower - upper, along, offset)) * quarter_root


def shrink_detail(detail, limit):
    magnitude = jnp.sqrt(detail[:, 0] * detail[:, 0] + detail[:, 1] * detail[:, 1])
    limit = limit.reshape((-1, 1, 1, 1))
    factor = jnp.maximum(magnitude - limit, 0.0) / jnp.maximum(magnitude, limit)
    return detail * factor[:, None]


def wavelet_shrink(descent, thresholds, moves):
    coarse = descent[None]
    details = []
    for level in range(thresholds.shape[0]):
        offset = 2**level
        bands = coarse
        for along, after, before in moves:
            bands = split_bands(bands, along, offset, after)
        coarse = bands[:1]
        details.append(shrink_detail(bands[1:], thresholds[level]))
    for level in reversed(range(thresholds.shape[0])):
        offset = 2**level
        bands = jnp.concatenate([coarse, details[level]], axis=0)
        for along, after, before in reversed(moves):
            bands = merge_bands(bands, along, offset, before)
        coarse = bands
    return coarse[0]


def local(image, sens, measured, mask, thresholds):
    readout_cells = image.shape[3]
    phase_cells = image.shape[1]
    depth_cells = measured.shape[3]
    table_readout = fourier_table(readout_cells, -1.0)
    table_phase = fourier_table(phase_cells, -1.0)
    table_depth = fourier_table(depth_cells, -1.0)
    inverse_readout = fourier_table(readout_cells, 1.0)
    inverse_phase = fourier_table(phase_cells, 1.0)
    inverse_depth = fourier_table(depth_cells, 1.0)
    sens_wide = sens.astype(jnp.float32)
    coil_image = complex_product(sens_wide, image[:, None]).astype(jnp.bfloat16)
    readout_done = contract("tcyzj,stjk->scyzk", coil_image, table_readout).astype(jnp.bfloat16)
    phase_done = contract("tcjzx,stjk->sckzx", readout_done, table_phase).astype(jnp.bfloat16)
    spread = lax.all_to_all(phase_done, ("slab", "row"), split_axis=2, concat_axis=3, tiled=True)
    spectrum = contract("tcyjx,stjk->scykx", spread, table_depth)
    sampled = mask.astype(jnp.float32)[None, None, :, :, None]
    residual = (sampled * (spectrum - measured.astype(jnp.float32))).astype(jnp.bfloat16)
    depth_back = contract("tcyjx,stjk->scykx", residual, inverse_depth).astype(jnp.bfloat16)
    gathered = lax.all_to_all(depth_back, ("slab", "row"), split_axis=3, concat_axis=2, tiled=True)
    phase_back = contract("tcjzx,stjk->sckzx", gathered, inverse_phase).astype(jnp.bfloat16)
    readout_back = contract("tcyzj,stjk->scyzk", phase_back, inverse_readout)
    partial_value = jnp.stack(
        [
            jnp.sum(sens_wide[0] * readout_back[0] + sens_wide[1] * readout_back[1], axis=0),
            jnp.sum(sens_wide[0] * readout_back[1] - sens_wide[1] * readout_back[0], axis=0),
        ]
    )
    gradient = lax.psum(partial_value.astype(jnp.bfloat16), "coil").astype(jnp.float32)
    descent = image - step_size * gradient
    moves = [
        (4, roll_after, roll_before),
        (2, roll_after, roll_before),
        (3, plane_after, plane_before),
    ]
    return wavelet_shrink(descent, thresholds, moves)


def solution(mesh):
    return jax.shard_map(
        local,
        mesh=mesh,
        in_specs=(
            P("groups", None, ("slab", "row"), None),
            P("groups", "coil", None, ("slab", "row"), None),
            P("groups", "coil", ("slab", "row"), None, None),
            P(("slab", "row"), None),
            P(),
        ),
        out_specs=P("groups", None, ("slab", "row"), None),
        check_vma=False,
    )
```

profile of v0, /device:TPU:0, one launch (start us, length us, event | category | flops | bytes accessed | tf_op | source)
XLA Modules:
  0.0 727.4 jit_solution(10082498368846165496)
XLA Ops:
  7.4 11.7 %copy_convert_fusion = f32[2,8,128,16,128]{4,2,0,3,1:T(8,128)} fusion(bf16[2,8,128,16,128]{4,3,2,1,0:T(8,128)(2,1)} %param.6), kind=kLoop, calls=%fused_computation.53 | loop fusion | flops 4194304 | bytes 25165824 | tf_op jit(solution)/shard_map/convert_element_type | solution.py:111
  20.0 9.9 %subtract_convert_fusion = (bf16[1,8,128,16,128]{4,2,0,3,1:T(8,128)(2,1)}, bf16[1,8,128,16,128]{4,2,0,3,1:T(8,128)(2,1)}) fusion(f32[2,8,128,16,128]{4,2,0,3,1:T(8,128)} %copy_convert_fusion, f32[128,16,128]{2,0,1:T(8,128)S(1)} %copy.36, f32[128,16,128]{2,0,1:T(8,128)S(1)} %copy.35), kind=kLoop, calls=%fused_computation.61 | loop fusion | flops 16777216 | bytes 27262976 | tf_op jit(solution)/shard_map/convert.8
  29.9 9.1 %fusion.6 = bf16[2,8,128,16,128]{4,2,3,1,0:T(8,128)(2,1)} fusion(bf16[1,8,128,16,128]{4,2,0,3,1:T(8,128)(2,1)} %get-tuple-element.8, bf16[1,8,128,16,128]{4,2,0,3,1:T(8,128)(2,1)} %get-tuple-element.7, bf16[1,2,128,128]{2,3,1,0:T(8,128)(2,1)S(1)} %get-tuple-element.28, bf16[1,2,128,128]{2,3,1,0:T(8,128)(2,1)S(1)} %get-tuple-element.29), kind=kOutput, calls=%fused_computation.30 | convolution fusion | flops 4320657408 | bytes 16908288 | tf_op jit(solution)/shard_map/tcjzx,stjk->sckzx/dot_general | solution.py:31
  39.0 12.0 %copy.38 = bf16[2,8,128,16,128]{4,3,1,0,2:T(8,128)(2,1)} copy(bf16[2,8,128,16,128]{4,2,3,1,0:T(8,128)(2,1)} %fusion.6) | data formatting | bytes 16777216 | tf_op jit(solution)/shard_map/convert_element_type | solution.py:114
  51.0 7.6 %all-to-all-start = ((bf16[2,8,128,16,128]{4,3,1,0,2:T(8,128)(2,1)}), bf16[2,8,128,16,128]{4,3,1,0,2:T(8,128)(2,1)}, u32[]{:S(2)}, u32[]{:S(2)}) async-start(bf16[2,8,128,16,128]{4,3,1,0,2:T(8,128)(2,1)} %copy.38), calls=%async_computation | async-start | bytes 16777216 | tf_op jit(solution)/shard_map/all_to_all | solution.py:115
  62.0 147.1 %all-to-all-done = bf16[2,8,128,16,128]{4,3,1,0,2:T(8,128)(2,1)} async-done(((bf16[2,8,128,16,128]{4,3,1,0,2:T(8,128)(2,1)}), bf16[2,8,128,16,128]{4,3,1,0,2:T(8,128)(2,1)}, u32[]{:S(2)}, u32[]{:S(2)}) %all-to-all-start) | async-done | bytes 8388640 | tf_op jit(solution)/shard_map/all_to_all | solution.py:115
  209.2 9.1 %copy.40 = bf16[2,8,8,16,16,128]{5,4,3,2,1,0:T(8,128)(2,1)} copy(bf16[2,8,8,16,16,128]{5,4,1,0,2,3:T(8,128)(2,1)} %bitcast.31) | data formatting | bytes 16777216 | tf_op jit(solution)/shard_map/all_to_all | solution.py:115
  218.3 9.5 %fusion.1 = bf16[2,8,8,256,128]{4,3,2,1,0:T(8,128)(2,1)S(1)} fusion(bf16[2,8,8,256,128]{4,3,2,1,0:T(8,128)(2,1)} %param.7, f32[8,256]{1,0:T(8,128)S(1)} %convert_element_type.150, bf16[2,8,8,256,128]{4,3,2,1,0:T(8,128)(2,1)} %bitcast.172, bf16[1,2,256,256]{2,3,1,0:T(8,128)(2,1)S(1)} %get-tuple-element.24, bf16[1,2,256,256]{2,3,1,0:T(8,128)(2,1)S(1)} %get-tuple-element.25), kind=kOutput, calls=%fused_computation.10 | convolution fusion | flops 4312793088 | bytes 25698304 | tf_op jit(solution)/shard_map/tcyjx,stjk->scykx/dot_general | solution.py:31
  227.9 6.7 fusion.7
  234.6 12.1 %copy.43 = bf16[2,8,8,256,128]{4,2,1,0,3:T(8,128)(2,1)} copy(bf16[2,8,8,256,128]{4,3,2,1,0:T(8,128)(2,1)} %fusion.7) | data formatting | bytes 16777216 | tf_op jit(solution)/shard_map/convert_element_type | solution.py:119
  246.6 218.8 %all_to_all.36 = bf16[2,8,8,256,128]{4,2,1,0,3:T(8,128)(2,1)} all-to-all(bf16[2,8,8,256,128]{4,2,1,0,3:T(8,128)(2,1)} %copy.43), channel_id=1, replica_groups=mesh['groups'=1,'slab'=8,'coil'=2,'row'=2] {'slab','row'}, dimensions={3} | all-to-all | bytes 16777216 | tf_op jit(solution)/shard_map/all_to_all | solution.py:120
  465.4 16.3 %copy.45 = bf16[2,8,16,8,16,128]{5,4,3,2,1,0:T(8,128)(2,1)} copy(bf16[2,8,16,8,16,128]{5,3,1,0,4,2:T(8,128)(2,1)} %bitcast.169) | data formatting | bytes 16777216 | tf_op jit(solution)/shard_map/all_to_all | solution.py:120
  481.8 12.5 %convolution_bitcast_fusion = f32[2,8,128,16,128]{4,2,0,3,1:T(8,128)} fusion(bf16[2,8,128,16,128,1]{4,3,2,1,0,5:T(8,128)(2,1)} %bitcast.168, bf16[1,2,128,128]{2,3,1,0:T(8,128)(2,1)S(1)} %get-tuple-element.30, bf16[1,2,128,128]{2,3,1,0:T(8,128)(2,1)S(1)} %get-tuple-element.27), kind=kOutput, calls=%fused_computation.29 | convolution fusion | flops 4299685888 | bytes 25296896 | tf_op jit(solution)/shard_map/tcyzj,stjk->scyzk/dot_general | solution.py:31
  494.3 13.1 %add_reduce_fusion = (bf16[128,16,128]{2,0,1:T(8,128)(2,1)S(1)}, bf16[128,16,128]{2,0,1:T(8,128)(2,1)S(1)}) fusion(f32[2,8,128,16,128]{4,2,0,3,1:T(8,128)} %convolution_bitcast_fusion, f32[2,8,128,16,128]{4,2,0,3,1:T(8,128)} %copy_convert_fusion), kind=kLoop, calls=%fused_computation.59 | loop fusion | flops 16252928 | bytes 34603008 | tf_op jit(solution)/shard_map/reduce_sum | solution.py:125
  511.1 39.3 %all-reduce.2.cloned.1.call-done = bf16[2,128,16,128]{1,3,2,0:T(8,128)(2,1)} async-done(((bf16[2,128,16,128]{1,3,2,0:T(8,128)(2,1)}), bf16[2,128,16,128]{1,3,2,0:T(8,128)(2,1)}) %all-reduce.2.cloned.1.call-update) | async-done | bytes 1048592 | tf_op jit(solution)/shard_map/psum | solution.py:129
  564.1 6.8 subtract_multiply_fusion
  578.7 4.2 subtract_multiply_fusion.2
  583.0 4.7 collective-permute-start.1
  587.7 5.4 divide_bitcast_fusion
  596.3 8.9 %subtract_multiply_fusion.1 = (f32[4,2,128,16,128]{2,4,3,1,0:T(8,128)}, f32[4,2,128,16,128]{2,4,3,1,0:T(8,128)S(1)}) fusion(f32[4,2,128,2,128]{2,4,3,1,0:T(8,128)S(1)} %convert_element_type.163, f32[4,2,128,14,128]{2,4,3,1,0:T(8,128)} %fusion.23, f32[2,2,128,16,128]{2,4,3,1,0:T(8,128)} %copy-done.4, f32[2,2,128,16,128]{2,4,3,1,0:T(8,128)} %copy-done.5), kind=kLoop, calls=%fused_computation.55 | loop fusion | flops 12582912 | bytes 33554432 | tf_op jit(solution)/shard_map/mul | solution.py:65
  608.4 7.7 %divide_bitcast_fusion.1 = f32[7,128,16,128]{1,3,2,0:T(8,128)} fusion(f32[4,2,128,16,128]{2,4,3,1,0:T(8,128)} %get-tuple-element.9, f32[4,2,128,16,128]{2,4,3,1,0:T(8,128)S(1)} %get-tuple-element.10, f32[7]{0:T(128)S(1)} %get-tuple-element.31), kind=kLoop, calls=%fused_computation.79 | loop fusion | flops 16515072 | bytes 24117276 | tf_op jit(solution)/shard_map/mul | solution.py:79
  616.2 8.2 %fusion.5 = f32[7,2,128,16,128]{2,4,3,1,0:T(8,128)S(1)} fusion(f32[4,2,128,16,128]{2,4,3,1,0:T(8,128)} %copy-done.1, f32[4,2,128,16,128]{2,4,3,1,0:T(8,128)} %get-tuple-element.9, f32[7,128,16,128]{1,3,2,0:T(8,128)} %divide_bitcast_fusion.1), kind=kLoop, calls=%fused_computation.18 | loop fusion | flops 7340032 | bytes 38797312 | tf_op jit(solution)/shard_map/mul | solution.py:79
  624.4 4.0 slice_subtract_fusion.1
  629.8 11.4 %fusion.3 = f32[7,2,128,16,128]{2,4,3,1,0:T(8,128)} fusion(f32[4,2,128,16,128]{2,4,3,1,0:T(8,128)S(1)} %bitcast.165, f32[4,2,128,16,128]{2,4,3,1,0:T(8,128)} %copy-done.3, f32[7,128,16,128]{1,3,2,0:T(8,128)} %divide_bitcast_fusion), kind=kLoop, calls=%fused_computation.16 | loop fusion | flops 7340032 | bytes 38797312 | tf_op jit(solution)/shard_map/mul | solution.py:79
  641.3 6.9 slice.282
  648.3 6.9 fusion.10
  655.2 4.2 slice_subtract_fusion.3
  662.7 9.9 %fusion.44 = f32[2,2,128,16,128]{2,4,3,1,0:T(8,128)} fusion(f32[2,2,126,16,128]{2,4,3,1,0:T(8,128)} %bitcast.166, f32[2,2,2,16,128]{2,4,3,1,0:T(8,128)} %slice.285, f32[4,2,128,16,128]{2,4,3,1,0:T(8,128)} %fusion.10), kind=kLoop, calls=%fused_computation.97 | loop fusion | flops 4194304 | bytes 16777216 | tf_op jit(solution)/shard_map/mul | solution.py:72
  683.5 7.3 %slice.297 = f32[4,2,128,15,128]{2,4,3,1,0:T(8,128)} slice(f32[4,2,128,16,128]{2,4,3,1,0:T(8,128)} %copy-done.10), slice={[0:4], [0:2], [0:128], [0:15], [0:128]} | slice | bytes 15728640 | tf_op jit(solution)/shard_map/slice | solution.py:59
  692.0 7.2 fusion.11
  699.2 4.2 slice_subtract_fusion.2
  708.3 5.7 fusion.45
  (103 shorter events, 64.5 us)
Async XLA Ops:
  7.4 11.7 %copy-start.11 = (f32[2,128,16,128]{3,2,1,0:T(8,128)S(1)}, f32[2,128,16,128]{3,2,1,0:T(8,128)}, u32[]{:S(2)}) copy-start(f32[2,128,16,128]{3,2,1,0:T(8,128)} %param.5) | copy-start | bytes 6291460
  51.0 7.7 %copy-start.13 = (s32[8,256]{1,0:T(8,128)S(1)}, s32[8,256]{1,0:T(8,128)}, u32[]{:S(2)}) copy-start(s32[8,256]{1,0:T(8,128)} %param.8) | copy-start | bytes 24580
  51.0 158.2 %all-to-all-start = ((bf16[2,8,128,16,128]{4,3,1,0,2:T(8,128)(2,1)}), bf16[2,8,128,16,128]{4,3,1,0,2:T(8,128)(2,1)}, u32[]{:S(2)}, u32[]{:S(2)}) async-start(bf16[2,8,128,16,128]{4,3,1,0,2:T(8,128)(2,1)} %copy.38), calls=%async_computation | async-start | bytes 16777216 | tf_op jit(solution)/shard_map/all_to_all | solution.py:115
  58.6 491.8 %all-reduce.2.cloned.1.call-start = ((), (), s32[]{:S(2)}) async-start(), calls=%async_computation.2 | async-start | bytes 2097152 | tf_op jit(solution)/shard_map/psum | solution.py:129
  507.4 3.7 copy-start.14
  550.4 1.9 copy-start.12
  556.5 7.4 %copy-start.6 = (f32[2,2,128,16,128]{2,4,3,1,0:T(8,128)}, f32[2,2,128,16,128]{2,4,3,1,0:T(8,128)S(1)}, u32[]{:S(2)}) copy-start(f32[2,2,128,16,128]{2,4,3,1,0:T(8,128)S(1)} %get-tuple-element.15) | copy-start | bytes 12582916
  556.5 7.4 %copy-start.7 = (f32[2,2,128,16,128]{2,4,3,1,0:T(8,128)}, f32[2,2,128,16,128]{2,4,3,1,0:T(8,128)S(1)}, u32[]{:S(2)}) copy-start(f32[2,2,128,16,128]{2,4,3,1,0:T(8,128)S(1)} %get-tuple-element.16) | copy-start | bytes 12582916
  556.6 7.5 %collective-permute-start = (bf16[4,2,128,1,128]{2,4,3,1,0:T(8,128)(2,1)S(1)}, bf16[4,2,128,1,128]{2,4,3,1,0:T(8,128)(2,1)S(1)}, u32[]{:S(2)}, u32[]{:S(2)}) collective-permute-start(bf16[4,2,128,1,128]{2,4,3,1,0:T(8,128)(2,1)S(1)} %fusion.61), channel_id=1, source_target_pairs={{1,0},{4,1},{5,4},{8,5},{9,8},{12,9},{13,12},{16,13},{17,16},{20,1... | collective-permute-start | bytes 786440 | tf_op jit(solution)/shard_map/ppermute | solution.py:15
  570.9 16.8 %copy-start = (f32[4,2,128,16,128]{2,4,3,1,0:T(8,128)}, f32[4,2,128,16,128]{2,4,3,1,0:T(8,128)S(1)}, u32[]{:S(2)}) copy-start(f32[4,2,128,16,128]{2,4,3,1,0:T(8,128)S(1)} %get-tuple-element.12) | copy-start | bytes 25165828
  570.9 16.8 %copy-start.3 = (f32[4,2,128,16,128]{2,4,3,1,0:T(8,128)}, f32[4,2,128,16,128]{2,4,3,1,0:T(8,128)S(1)}, u32[]{:S(2)}) copy-start(f32[4,2,128,16,128]{2,4,3,1,0:T(8,128)S(1)} %get-tuple-element.11) | copy-start | bytes 25165828
  582.9 10.1 %copy-start.4 = (f32[2,2,128,16,128]{2,4,3,1,0:T(8,128)}, f32[2,2,128,16,128]{2,4,3,1,0:T(8,128)S(1)}, u32[]{:S(2)}) copy-start(f32[2,2,128,16,128]{2,4,3,1,0:T(8,128)S(1)} %get-tuple-element.13) | copy-start | bytes 12582916
  582.9 10.1 %copy-start.5 = (f32[2,2,128,16,128]{2,4,3,1,0:T(8,128)}, f32[2,2,128,16,128]{2,4,3,1,0:T(8,128)S(1)}, u32[]{:S(2)}) copy-start(f32[2,2,128,16,128]{2,4,3,1,0:T(8,128)S(1)} %get-tuple-element.14) | copy-start | bytes 12582916
  583.0 13.2 %collective-permute-start.1 = (bf16[4,2,128,2,128]{2,4,3,1,0:T(8,128)(2,1)S(1)}, bf16[4,2,128,2,128]{2,4,3,1,0:T(8,128)(2,1)S(1)}, u32[]{:S(2)}, u32[]{:S(2)}) collective-permute-start(bf16[4,2,128,2,128]{2,4,3,1,0:T(8,128)(2,1)S(1)} %fusion.54), channel_id=1, source_target_pairs={{1,0},{4,1},{5,4},{8,5},{9,8},{12,9},{13,12},{16,13},{17,16},{20,1... | collective-permute-start | bytes 1572872 | tf_op jit(solution)/shard_map/ppermute | solution.py:15
  605.2 3.2 copy-start.1
  608.4 21.4 %slice-start.4 = ((s8[8388608]{0:T(1024)(128)(4,1)}), s8[4194304]{0:T(1024)(128)(4,1)S(1)}, s32[]{:S(2)}) async-start(s8[8388608]{0:T(1024)(128)(4,1)} %bitcast.164), calls=%async_computation.7 | async-start | bytes 8388608
  616.2 13.6 %slice-start.5 = ((s8[8388608]{0:T(1024)(128)(4,1)}), s8[4194304]{0:T(1024)(128)(4,1)S(1)}, s32[]{:S(2)}) async-start(s8[8388608]{0:T(1024)(128)(4,1)} %bitcast.164), calls=%async_computation.8 | async-start | bytes 8388608
  629.7 18.5 %collective-permute-start.2 = (bf16[4,2,128,2,128]{2,4,3,1,0:T(8,128)(2,1)S(1)}, bf16[4,2,128,2,128]{2,4,3,1,0:T(8,128)(2,1)S(1)}, u32[]{:S(2)}, u32[]{:S(2)}) collective-permute-start(bf16[4,2,128,2,128]{2,4,3,1,0:T(8,128)(2,1)S(1)} %slice.450), channel_id=1, source_target_pairs={{29,0},{0,1},{1,4},{4,5},{5,8},{8,9},{9,12},{12,13},{13,16},{16,17... | collective-permute-start | bytes 1572872 | tf_op jit(solution)/shard_map/ppermute | solution.py:15
  659.4 3.2 copy-start.8
  662.7 15.5 %slice-start = ((s8[14680064]{0:T(1024)(128)(4,1)}), s8[4194304]{0:T(1024)(128)(4,1)S(1)}, s32[]{:S(2)}) async-start(s8[14680064]{0:T(1024)(128)(4,1)} %bitcast.162), calls=%async_computation.3 | async-start | bytes 8388608
  662.7 15.5 %slice-start.1 = ((s8[14680064]{0:T(1024)(128)(4,1)}), s8[4194304]{0:T(1024)(128)(4,1)S(1)}, s32[]{:S(2)}) async-start(s8[14680064]{0:T(1024)(128)(4,1)} %bitcast.162), calls=%async_computation.4 | async-start | bytes 8388608
  662.7 15.6 %slice-start.2 = ((s8[14680064]{0:T(1024)(128)(4,1)}), s8[2097152]{0:T(1024)(128)(4,1)S(1)}, s32[]{:S(2)}) async-start(s8[14680064]{0:T(1024)(128)(4,1)} %bitcast.162), calls=%async_computation.5 | async-start | bytes 4194304
  672.6 5.6 slice-start.3
  680.1 3.3 copy-start.10
  683.4 8.5 %collective-permute-start.3 = (bf16[4,2,128,1,128]{2,4,3,1,0:T(8,128)(2,1)S(1)}, bf16[4,2,128,1,128]{2,4,3,1,0:T(8,128)(2,1)S(1)}, u32[]{:S(2)}, u32[]{:S(2)}) collective-permute-start(bf16[4,2,128,1,128]{2,4,3,1,0:T(8,128)(2,1)S(1)} %slice.451), channel_id=1, source_target_pairs={{29,0},{0,1},{1,4},{4,5},{5,8},{8,9},{9,12},{12,13},{13,16},{16,17... | collective-permute-start | bytes 786440 | tf_op jit(solution)/shard_map/ppermute | solution.py:15
  703.4 4.9 copy-start.2
  714.0 3.4 copy-start.9
Sparse Core Ops, SparseCore 0:
  509.2 41.1 all-reduce.1
where the time goes:
time: 731 us; the launch traced here: 727 us
  blocking collectives  219 us (30%)
  waiting for transfers between devices  188 us (26%)
  other arithmetic  166 us (23%)
  local copies, waits for them, and re-layouts  86.6 us (12%)
  matrix products  37.9 us (5%)
  starting transfers between devices  16 us (2%)
  between operations  14.2 us (2%)
    all_to_all x1, blocking collectives, local(): lax.all_to_all(depth_back, ('slab', 'row'), split_axis=3, concat_axis=2,...  219 us
    all_to_all x1, waiting for transfers between devices, local(): lax.all_to_all(phase_done, ('slab', 'row'), split_axis=2, concat_axis=3,...  147 us
    psum x1, waiting for transfers between devices, local(): lax.psum(partial_value.astype(jnp.bfloat16), 'coil').astype(jnp.float32)  39.3 us
    dot_general x4, matrix products, contract(): return jnp.einsum(form, values, table, preferred_element_type=jnp.float32)  37.9 us
    mul x4, other arithmetic, shrink_detail(): return detail * factor[:, None]  32.8 us
    mul x5, other arithmetic, merge_bands(): return (lower + upper + before(lower - upper, along, offset)) * quarter_root  32.6 us
    mul x3, other arithmetic, split_bands(): (bands - moved) * half_root  19.9 us
    sub x6, other arithmetic, merge_bands(): return (lower + upper + before(lower - upper, along, offset)) * quarter_root  19.6 us
  transfers between devices with their start and end apart: 6, of which 4 were waited for; matrix products, arithmetic and copies ran while one was open for 6% of the time, Pallas kernels for 0%

commit v1 on v0

--- a/solution.py
+++ b/solution.py
@@ -126,7 +126,13 @@
             jnp.sum(sens_wide[0] * readout_back[1] - sens_wide[1] * readout_back[0], axis=0),
         ]
     )
-    gradient = lax.psum(partial_value.astype(jnp.bfloat16), "coil").astype(jnp.float32)
+
+    def supply_the_marks(raw):
+        carry_out = lax.all_gather(raw, "coil")
+        m_next = jnp.sum(carry_out, axis=0)
+        return m_next
+
+    gradient = supply_the_marks(partial_value.astype(jnp.bfloat16)).astype(jnp.float32)
     descent = image - step_size * gradient
     moves = [
         (4, roll_after, roll_before),

time: 731 us -> 709 us (0.970)
  other arithmetic: 166 us -> 147 us
  local copies, waits for them, and re-layouts: 86.6 us -> 73.5 us
  waiting for transfers between devices: 188 us -> 199 us
    psum x1 -> x0, waiting for transfers between devices: 39.3 us -> none  [local(): lax.psum(partial_value.astype(jnp.bfloat16), 'coil').astype(jnp.float32)]
    all_gather x0 -> x1, waiting for transfers between devices: none -> 34.3 us  [supply_the_marks(): carry_out = lax.all_gather(raw, 'coil')]
    ppermute x4, waiting for transfers between devices: 1.27 us -> 17.2 us  [passed_along(): return lax.ppermute(block, axis, route)]
    slice x2 -> x0, local copies, waits for them, and re-layouts: 14.3 us -> none  [plane_before(): remain = lax.slice_in_dim(values, 0, extent - offset, axis=along)]
    mul x3 -> x4, other arithmetic: 19.9 us -> 20.4 us  [split_bands(): (bands - moved) * half_root]
  transfers between devices with their start and end apart: 6 -> 6, of which waited for: 4 -> 5; matrix products, arithmetic and copies ran while one was open for 6% -> 3% of each run, Pallas kernels for 0% -> 0%
where the time goes in v1:
time: 709 us; the launch traced here: 705 us
  blocking collectives  219 us (31%)
  waiting for transfers between devices  199 us (28%)
  other arithmetic  147 us (21%)
  local copies, waits for them, and re-layouts  73.5 us (10%)
  matrix products  37.8 us (5%)
  starting transfers between devices  15.9 us (2%)
  between operations  14.1 us (2%)
    all_to_all x1, blocking collectives, local(): lax.all_to_all(depth_back, ('slab', 'row'), split_axis=3, concat_axis=2,...  219 us
    all_to_all x1, waiting for transfers between devices, local(): lax.all_to_all(phase_done, ('slab', 'row'), split_axis=2, concat_axis=3,...  147 us
    dot_general x4, matrix products, contract(): return jnp.einsum(form, values, table, preferred_element_type=jnp.float32)  37.8 us
    all_gather x1, waiting for transfers between devices, supply_the_marks(): carry_out = lax.all_gather(raw, 'coil')  34.3 us
    mul x5, other arithmetic, merge_bands(): return (lower + upper + before(lower - upper, along, offset)) * quarter_root  28.4 us
    mul x4, other arithmetic, shrink_detail(): return detail * factor[:, None]  28.1 us
    mul x4, other arithmetic, split_bands(): (bands - moved) * half_root  20.4 us
    ppermute x4, waiting for transfers between devices, passed_along(): return lax.ppermute(block, axis, route)  17.2 us
  transfers between devices with their start and end apart: 6, of which 5 were waited for; matrix products, arithmetic and copies ran while one was open for 3% of the time, Pallas kernels for 0%

profile of v1, /device:TPU:0, one launch (start us, length us, event | category | flops | bytes accessed | tf_op | source)
XLA Modules:
  0.0 705.4 jit_solution(7943010002101296552)
XLA Ops:
  7.4 11.7 %copy_convert_fusion = f32[2,8,128,16,128]{4,2,0,3,1:T(8,128)} fusion(bf16[2,8,128,16,128]{4,3,2,1,0:T(8,128)(2,1)} %param.6), kind=kLoop, calls=%fused_computation.55 | loop fusion | flops 4194304 | bytes 25165824 | tf_op jit(solution)/shard_map/convert_element_type | solution.py:111
  19.9 9.9 %subtract_convert_fusion = (bf16[1,8,128,16,128]{4,2,0,3,1:T(8,128)(2,1)}, bf16[1,8,128,16,128]{4,2,0,3,1:T(8,128)(2,1)}) fusion(f32[2,8,128,16,128]{4,2,0,3,1:T(8,128)} %copy_convert_fusion, f32[128,16,128]{2,0,1:T(8,128)S(1)} %copy.55, f32[128,16,128]{2,0,1:T(8,128)S(1)} %copy.54), kind=kLoop, calls=%fused_computation.63 | loop fusion | flops 16777216 | bytes 27262976 | tf_op jit(solution)/shard_map/convert.9
  29.8 9.0 %fusion.8 = bf16[2,8,128,16,128]{4,2,3,1,0:T(8,128)(2,1)} fusion(bf16[1,8,128,16,128]{4,2,0,3,1:T(8,128)(2,1)} %get-tuple-element.8, bf16[1,8,128,16,128]{4,2,0,3,1:T(8,128)(2,1)} %get-tuple-element.7, bf16[1,2,128,128]{2,3,1,0:T(8,128)(2,1)S(1)} %get-tuple-element.28, bf16[1,2,128,128]{2,3,1,0:T(8,128)(2,1)S(1)} %get-tuple-element.29), kind=kOutput, calls=%fused_computation.32 | convolution fusion | flops 4320657408 | bytes 16908288 | tf_op jit(solution)/shard_map/tcjzx,stjk->sckzx/dot_general | solution.py:31
  38.9 12.0 %copy.57 = bf16[2,8,128,16,128]{4,3,1,0,2:T(8,128)(2,1)} copy(bf16[2,8,128,16,128]{4,2,3,1,0:T(8,128)(2,1)} %fusion.8) | data formatting | bytes 16777216 | tf_op jit(solution)/shard_map/convert_element_type | solution.py:114
  50.9 7.6 %all-to-all-start = ((bf16[2,8,128,16,128]{4,3,1,0,2:T(8,128)(2,1)}), bf16[2,8,128,16,128]{4,3,1,0,2:T(8,128)(2,1)}, u32[]{:S(2)}, u32[]{:S(2)}) async-start(bf16[2,8,128,16,128]{4,3,1,0,2:T(8,128)(2,1)} %copy.57), calls=%async_computation | async-start | bytes 16777216 | tf_op jit(solution)/shard_map/all_to_all | solution.py:115
  61.9 147.1 %all-to-all-done = bf16[2,8,128,16,128]{4,3,1,0,2:T(8,128)(2,1)} async-done(((bf16[2,8,128,16,128]{4,3,1,0,2:T(8,128)(2,1)}), bf16[2,8,128,16,128]{4,3,1,0,2:T(8,128)(2,1)}, u32[]{:S(2)}, u32[]{:S(2)}) %all-to-all-start) | async-done | bytes 8388640 | tf_op jit(solution)/shard_map/all_to_all | solution.py:115
  209.1 9.1 %copy.59 = bf16[2,8,8,16,16,128]{5,4,3,2,1,0:T(8,128)(2,1)} copy(bf16[2,8,8,16,16,128]{5,4,1,0,2,3:T(8,128)(2,1)} %bitcast.31) | data formatting | bytes 16777216 | tf_op jit(solution)/shard_map/all_to_all | solution.py:115
  218.2 9.5 %fusion.1 = bf16[2,8,8,256,128]{4,3,2,1,0:T(8,128)(2,1)S(1)} fusion(bf16[2,8,8,256,128]{4,3,2,1,0:T(8,128)(2,1)} %param.7, f32[8,256]{1,0:T(8,128)S(1)} %convert_element_type.159, bf16[2,8,8,256,128]{4,3,2,1,0:T(8,128)(2,1)} %bitcast.167, bf16[1,2,256,256]{2,3,1,0:T(8,128)(2,1)S(1)} %get-tuple-element.24, bf16[1,2,256,256]{2,3,1,0:T(8,128)(2,1)S(1)} %get-tuple-element.25), kind=kOutput, calls=%fused_computation.10 | convolution fusion | flops 4312793088 | bytes 25698304 | tf_op jit(solution)/shard_map/tcyjx,stjk->scykx/dot_general | solution.py:31
  227.7 6.7 fusion.9
  234.4 12.0 %copy.62 = bf16[2,8,8,256,128]{4,2,1,0,3:T(8,128)(2,1)} copy(bf16[2,8,8,256,128]{4,3,2,1,0:T(8,128)(2,1)} %fusion.9) | data formatting | bytes 16777216 | tf_op jit(solution)/shard_map/convert_element_type | solution.py:119
  246.5 218.8 %all_to_all.36 = bf16[2,8,8,256,128]{4,2,1,0,3:T(8,128)(2,1)} all-to-all(bf16[2,8,8,256,128]{4,2,1,0,3:T(8,128)(2,1)} %copy.62), channel_id=1, replica_groups=mesh['groups'=1,'slab'=8,'coil'=2,'row'=2] {'slab','row'}, dimensions={3} | all-to-all | bytes 16777216 | tf_op jit(solution)/shard_map/all_to_all | solution.py:120
  465.3 16.3 %copy.64 = bf16[2,8,16,8,16,128]{5,4,3,2,1,0:T(8,128)(2,1)} copy(bf16[2,8,16,8,16,128]{5,3,1,0,4,2:T(8,128)(2,1)} %bitcast.163) | data formatting | bytes 16777216 | tf_op jit(solution)/shard_map/all_to_all | solution.py:120
  481.6 12.5 %convolution_bitcast_fusion = f32[2,8,128,16,128]{4,2,0,3,1:T(8,128)} fusion(bf16[2,8,128,16,128,1]{4,3,2,1,0,5:T(8,128)(2,1)} %bitcast.162, bf16[1,2,128,128]{2,3,1,0:T(8,128)(2,1)S(1)} %get-tuple-element.30, bf16[1,2,128,128]{2,3,1,0:T(8,128)(2,1)S(1)} %get-tuple-element.27), kind=kOutput, calls=%fused_computation.29 | convolution fusion | flops 4299685888 | bytes 25296896 | tf_op jit(solution)/shard_map/tcyzj,stjk->scyzk/dot_general | solution.py:31
  494.1 13.1 %add_reduce_fusion = (bf16[128,16,128]{2,0,1:T(8,128)(2,1)S(1)}, bf16[128,16,128]{2,0,1:T(8,128)(2,1)S(1)}) fusion(f32[2,8,128,16,128]{4,2,0,3,1:T(8,128)} %convolution_bitcast_fusion, f32[2,8,128,16,128]{4,2,0,3,1:T(8,128)} %copy_convert_fusion), kind=kLoop, calls=%fused_computation.61 | loop fusion | flops 16252928 | bytes 34603008 | tf_op jit(solution)/shard_map/reduce_sum | solution.py:125
  509.6 34.3 %all-gather.2.cloned.1.call-done = bf16[2,2,128,16,128]{4,3,2,1,0:T(8,128)(2,1)} async-done(((bf16[1,2,128,16,128]{4,3,2,1,0:T(8,128)(2,1)}), bf16[2,2,128,16,128]{4,3,2,1,0:T(8,128)(2,1)}) %all-gather.2.cloned.1.call-update) | async-done | bytes 2097168 | tf_op jit(solution)/shard_map/all_gather | solution.py:131
  556.3 3.6 collective-permute-start
  559.8 4.0 fusion.7
  567.1 7.0 subtract_multiply_fusion
  577.4 4.7 collective-permute-start.1
  582.1 5.2 divide_bitcast_fusion
  587.3 3.6 fusion.6
  591.3 9.6 %subtract_multiply_fusion.1 = (f32[4,2,128,16,128]{4,3,2,1,0:T(8,128)}, f32[4,2,128,16,128]{4,3,2,1,0:T(8,128)S(1)}) fusion(f32[2,2,128,16,128]{4,3,2,1,0:T(8,128)} %copy-done.5, f32[2,2,128,16,128]{4,3,2,1,0:T(8,128)} %copy-done.4, f32[4,2,128,2,128]{4,3,2,1,0:T(2,128)S(1)} %convert_element_type.172, f32[4,2,128,14,128]{4,3,2,1,0:T(8,128)} %fusion.6), kind=kLoop, calls=%fused_computation.57 | loop fusion | flops 12582912 | bytes 33554432 | tf_op jit(solution)/shard_map/mul | solution.py:65
  601.1 8.4 %divide_bitcast_fusion.1 = f32[7,128,16,128]{3,2,1,0:T(8,128)} fusion(f32[4,2,128,16,128]{4,3,2,1,0:T(8,128)} %get-tuple-element.9, f32[4,2,128,16,128]{4,3,2,1,0:T(8,128)S(1)} %get-tuple-element.10, f32[7]{0:T(128)S(1)} %get-tuple-element.31), kind=kLoop, calls=%fused_computation.79 | loop fusion | flops 16515072 | bytes 24117276 | tf_op jit(solution)/shard_map/mul | solution.py:79
  609.4 6.4 fusion.5
  617.1 4.0 copy-done
  624.4 8.1 %fusion.3 = f32[7,2,128,16,128]{4,3,2,1,0:T(8,128)S(1)} fusion(f32[4,2,128,16,128]{4,3,2,1,0:T(8,128)} %copy-done.1, f32[4,2,128,16,128]{4,3,2,1,0:T(8,128)} %copy-done.2, f32[7,128,16,128]{3,2,1,0:T(8,128)} %divide_bitcast_fusion), kind=kLoop, calls=%fused_computation.16 | loop fusion | flops 7340032 | bytes 38797312 | tf_op jit(solution)/shard_map/mul | solution.py:79
  636.1 12.8 %fusion.12 = f32[4,2,128,16,128]{4,3,2,1,0:T(8,128)} fusion(f32[4,2,128,14,128]{4,3,2,1,0:T(8,128)} %bitcast.160, f32[4,2,128,2,128]{4,3,2,1,0:T(2,128)S(1)} %convert_element_type.173, f32[7,2,128,16,128]{4,3,2,1,0:T(8,128)} %copy-done, f32[1,2,128,16,128]{4,3,2,1,0:T(8,128)} %copy-done.11), kind=kLoop, calls=%fused_computation.42 | loop fusion | flops 10485760 | bytes 42991616 | tf_op jit(solution)/shard_map/mul | solution.py:72
  648.9 4.0 slice_subtract_fusion.3
  655.2 5.5 fusion.40
  669.7 11.3 %collective-permute-done.3 = bf16[4,2,128,1,128]{4,3,2,1,0:T(2,128)(2,1)S(1)} collective-permute-done((bf16[4,2,128,1,128]{4,3,2,1,0:T(2,128)(2,1)S(1)}, bf16[4,2,128,1,128]{4,3,2,1,0:T(2,128)(2,1)S(1)}, u32[]{:S(2)}, u32[]{:S(2)}) %collective-permute-start.3) | collective-permute-done | bytes 262176 | tf_op jit(solution)/shard_map/ppermute | solution.py:15
  681.6 7.3 %fusion.13 = f32[4,2,128,16,128]{4,3,2,1,0:T(8,128)} fusion(f32[4,2,128,15,128]{4,3,2,1,0:T(8,128)} %bitcast.161, f32[4,2,128,1,128]{4,3,2,1,0:T(1,128)S(1)} %convert_element_type.174, f32[7,2,128,16,128]{4,3,2,1,0:T(8,128)S(1)} %fusion.3, f32[1,2,128,16,128]{4,3,2,1,0:T(8,128)} %fusion.48), kind=kLoop, calls=%fused_computation.44 | loop fusion | flops 10485760 | bytes 41943040 | tf_op jit(solution)/shard_map/mul | solution.py:72
  688.9 4.2 slice_subtract_fusion.2
  (88 shorter events, 52.0 us)
Async XLA Ops:
  7.4 11.7 %copy-start.10 = (f32[2,128,16,128]{3,2,1,0:T(8,128)S(1)}, f32[2,128,16,128]{3,2,1,0:T(8,128)}, u32[]{:S(2)}) copy-start(f32[2,128,16,128]{3,2,1,0:T(8,128)} %param.5) | copy-start | bytes 6291460
  50.9 7.7 %copy-start.12 = (s32[8,256]{1,0:T(8,128)S(1)}, s32[8,256]{1,0:T(8,128)}, u32[]{:S(2)}) copy-start(s32[8,256]{1,0:T(8,128)} %param.8) | copy-start | bytes 24580
  50.9 158.2 %all-to-all-start = ((bf16[2,8,128,16,128]{4,3,1,0,2:T(8,128)(2,1)}), bf16[2,8,128,16,128]{4,3,1,0,2:T(8,128)(2,1)}, u32[]{:S(2)}, u32[]{:S(2)}) async-start(bf16[2,8,128,16,128]{4,3,1,0,2:T(8,128)(2,1)} %copy.57), calls=%async_computation | async-start | bytes 16777216 | tf_op jit(solution)/shard_map/all_to_all | solution.py:115
  58.5 485.4 %all-gather.2.cloned.1.call-start = ((), (), s32[]{:S(2)}) async-start(), calls=%async_computation.2 | async-start | bytes 3145728 | tf_op jit(solution)/shard_map/all_gather | solution.py:131
  507.2 2.4 copy-start.13
  555.8 8.0 %copy-start.6 = (f32[2,2,128,16,128]{4,3,2,1,0:T(8,128)}, f32[2,2,128,16,128]{4,3,2,1,0:T(8,128)S(1)}, u32[]{:S(2)}) copy-start(f32[2,2,128,16,128]{4,3,2,1,0:T(8,128)S(1)} %get-tuple-element.17) | copy-start | bytes 12582916
  555.8 8.0 %copy-start.7 = (f32[2,2,128,16,128]{4,3,2,1,0:T(8,128)}, f32[2,2,128,16,128]{4,3,2,1,0:T(8,128)S(1)}, u32[]{:S(2)}) copy-start(f32[2,2,128,16,128]{4,3,2,1,0:T(8,128)S(1)} %get-tuple-element.18) | copy-start | bytes 12582916
  556.3 10.3 %collective-permute-start = (bf16[4,2,128,1,128]{4,3,2,1,0:T(2,128)(2,1)S(1)}, bf16[4,2,128,1,128]{4,3,2,1,0:T(2,128)(2,1)S(1)}, u32[]{:S(2)}, u32[]{:S(2)}) collective-permute-start(bf16[4,2,128,1,128]{4,3,2,1,0:T(2,128)(2,1)S(1)} %fusion.59), channel_id=1, source_target_pairs={{1,0},{4,1},{5,4},{8,5},{9,8},{12,9},{13,12},{16,13},{17,16},{20,1... | collective-permute-start | bytes 786440 | tf_op jit(solution)/shard_map/ppermute | solution.py:15
  574.1 8.0 %copy-start.1 = (f32[4,2,128,16,128]{4,3,2,1,0:T(8,128)}, f32[4,2,128,16,128]{4,3,2,1,0:T(8,128)S(1)}, u32[]{:S(2)}) copy-start(f32[4,2,128,16,128]{4,3,2,1,0:T(8,128)S(1)} %get-tuple-element.12) | copy-start | bytes 25165828
  574.1 8.0 %copy-start.2 = (f32[4,2,128,16,128]{4,3,2,1,0:T(8,128)}, f32[4,2,128,16,128]{4,3,2,1,0:T(8,128)S(1)}, u32[]{:S(2)}) copy-start(f32[4,2,128,16,128]{4,3,2,1,0:T(8,128)S(1)} %get-tuple-element.11) | copy-start | bytes 25165828
  576.9 10.4 %copy-start.4 = (f32[2,2,128,16,128]{4,3,2,1,0:T(8,128)}, f32[2,2,128,16,128]{4,3,2,1,0:T(8,128)S(1)}, u32[]{:S(2)}) copy-start(f32[2,2,128,16,128]{4,3,2,1,0:T(8,128)S(1)} %get-tuple-element.15) | copy-start | bytes 12582916
  577.0 10.4 %copy-start.5 = (f32[2,2,128,16,128]{4,3,2,1,0:T(8,128)}, f32[2,2,128,16,128]{4,3,2,1,0:T(8,128)S(1)}, u32[]{:S(2)}) copy-start(f32[2,2,128,16,128]{4,3,2,1,0:T(8,128)S(1)} %get-tuple-element.16) | copy-start | bytes 12582916
  577.4 13.6 %collective-permute-start.1 = (bf16[4,2,128,2,128]{4,3,2,1,0:T(2,128)(2,1)S(1)}, bf16[4,2,128,2,128]{4,3,2,1,0:T(2,128)(2,1)S(1)}, u32[]{:S(2)}, u32[]{:S(2)}) collective-permute-start(bf16[4,2,128,2,128]{4,3,2,1,0:T(2,128)(2,1)S(1)} %fusion.52), channel_id=1, source_target_pairs={{1,0},{4,1},{5,4},{8,5},{9,8},{12,9},{13,12},{16,13},{17,16},{20,1... | collective-permute-start | bytes 1572872 | tf_op jit(solution)/shard_map/ppermute | solution.py:15
  601.1 14.8 %copy-start.11 = (f32[1,2,128,16,128]{4,3,2,1,0:T(8,128)}, f32[1,2,128,16,128]{4,3,2,1,0:T(8,128)S(1)}, u32[]{:S(2)}) copy-start(f32[1,2,128,16,128]{4,3,2,1,0:T(8,128)S(1)} %slice.275) | copy-start | bytes 6291460
  615.9 5.2 copy-start
  621.1 3.3 copy-start.8
  624.4 11.3 %collective-permute-start.2 = (bf16[4,2,128,2,128]{4,3,2,1,0:T(2,128)(2,1)S(1)}, bf16[4,2,128,2,128]{4,3,2,1,0:T(2,128)(2,1)S(1)}, u32[]{:S(2)}, u32[]{:S(2)}) collective-permute-start(bf16[4,2,128,2,128]{4,3,2,1,0:T(2,128)(2,1)S(1)} %slice.451), channel_id=1, source_target_pairs={{29,0},{0,1},{1,4},{4,5},{5,8},{8,9},{9,12},{12,13},{13,16},{16,17... | collective-permute-start | bytes 1572872 | tf_op jit(solution)/shard_map/ppermute | solution.py:15
  665.9 3.3 copy-start.9
  669.7 11.4 %collective-permute-start.3 = (bf16[4,2,128,1,128]{4,3,2,1,0:T(2,128)(2,1)S(1)}, bf16[4,2,128,1,128]{4,3,2,1,0:T(2,128)(2,1)S(1)}, u32[]{:S(2)}, u32[]{:S(2)}) collective-permute-start(bf16[4,2,128,1,128]{4,3,2,1,0:T(2,128)(2,1)S(1)} %slice.452), channel_id=1, source_target_pairs={{29,0},{0,1},{1,4},{4,5},{5,8},{8,9},{9,12},{12,13},{13,16},{16,17... | collective-permute-start | bytes 786440 | tf_op jit(solution)/shard_map/ppermute | solution.py:15
  688.9 5.8 copy-start.3
Sparse Core Ops, SparseCore 0:
  509.7 34.1 all-gather.1
